TPU v7x, 128 devices: a whole 4x4x4 slice. The times are simulated.
128 devices in a mesh: team: 8 (over x, core), inner: 16 (over z, y).
Axes of the slice: x: 4, y: 4, z: 4, core: 2. Of those that a mesh axis runs over, the one named last changes fastest.
Arguments:
- queries: float32 [16384, 1024], P(('team', 'inner')), may hold values from -8 to 8
- passages: float32 [16384, 1024], P(('team', 'inner')), may hold values from -8 to 8
- positive: int32 [16384], P(('team', 'inner')), may hold values from 0 to 16383, as said below
Outputs:
- grad_queries: float32 [16384, 1024], P(('team', 'inner'))
- grad_passages: float32 [16384, 1024], P(('team', 'inner'))
Inputs may be any that keep to these rules, and one draw needn't show every extreme that they name: `positive`: a permutation of the passage indices 0 to 16383.
All inputs are finite; a program needn't handle non-finite values.
Results may differ from a plain program's by a relative error of at most 0.014.
Values may be sent and summed in bfloat16 or wider, within the bound.
A program may use at most 64 MiB of HBM per device.

v0:
```python
import jax
import jax.numpy as jnp
from jax import lax
from jax.sharding import Mesh
from jax.sharding import PartitionSpec as P

INNER = ("inner_0", "inner_1")
TEAM_INNER = ("team", "inner_0", "inner_1")
logit_scale_factor = 20.0
epsilon = 1e-06


def in_order(blocks, dim):
    dims = list(blocks.shape[1:])
    dims[dim] *= blocks.shape[0]
    return jnp.moveaxis(blocks, 0, dim).reshape(dims)


def sent_to_all(x, axis):
    copies = jnp.broadcast_to(x, (lax.axis_size(axis), *x.shape))
    return lax.all_to_all(copies, axis, split_axis=0, concat_axis=0, tiled=True)


def gathered_copies(x, axis, dim):
    return in_order(sent_to_all(x, axis), dim)


def taken_together(x, axis):
    everything = sent_to_all(x, axis)
    return jnp.sum(everything, axis=0)


def summed_rows(terms, axes):
    so_far = terms.astype(jnp.bfloat16)
    for axis in axes:
        so_far = lax.psum_scatter(so_far, axis, scatter_dimension=0, tiled=True)
    return so_far.astype(jnp.float32)


def split_up(x, dim, size):
    dims = x.shape
    blocks = x.reshape(*dims[:dim], size, dims[dim] // size, *dims[dim + 1 :])
    return jnp.moveaxis(blocks, dim, 0)


def summed_on_arrival(x, axis, dim):
    size = lax.axis_size(axis)
    blocks = lax.all_to_all(split_up(x, dim, size), axis, 0, 0, tiled=True)
    return jnp.sum(blocks.astype(jnp.float32), axis=0)


def unit_rows(vectors):
    length = jnp.sqrt(jnp.sum(vectors * vectors, axis=1, keepdims=True) + epsilon)
    return (vectors / length, length)


def finish(unit_vectors, length, grad_raw):
    projection = jnp.sum(unit_vectors * grad_raw, axis=1, keepdims=True)
    return (grad_raw - unit_vectors * projection) / length


def exponent(query_tile_rows, column_block):
    similarity_scores = lax.dot_general(
        query_tile_rows, column_block, (((1,), (1,)), ((), ())), preferred_element_type=jnp.float32
    )
    return jnp.exp(logit_scale_factor * similarity_scores)


def weights(query_tile_rows, column_block, target_block, row_block, column_block_total):
    exponentials = exponent(query_tile_rows, column_block)
    column_ids = lax.iota(jnp.int32, column_block.shape[0])
    is_target = (target_block[:, None] == column_ids[None, :]).astype(jnp.float32)
    combined = (
        exponentials / row_block[:, None]
        + exponentials / column_block_total[None, :]
        - 2.0 * is_target
    )
    return combined.astype(jnp.bfloat16)


def per_device(queries, passages, positive):
    shard_rows = queries.shape[0]
    feature_count = queries.shape[1]
    inner_count = lax.axis_size(INNER)
    team_count = lax.axis_size("team")
    query_unit, query_length = unit_rows(queries)
    passage_unit, passage_length = unit_rows(passages)
    query_round = query_unit.astype(jnp.bfloat16)
    passage_round = passage_unit.astype(jnp.bfloat16)
    team_queries = lax.all_gather(query_round, INNER, axis=0, tiled=True)
    team_targets = lax.all_gather(positive, INNER, axis=0, tiled=True)
    columns = gathered_copies(passage_round, "team", 0)
    team_rows = shard_rows * inner_count
    column_count = shard_rows * team_count
    owner_inner = team_targets % team_rows // shard_rows
    target_column = team_targets // team_rows * shard_rows + team_targets % shard_rows
    target_column = jnp.where(owner_inner == lax.axis_index(INNER), target_column, -1)
    block_rows = shard_rows * min(inner_count, max(1, 512 // shard_rows))
    block_count = team_rows // block_rows
    query_blocks = team_queries.reshape(block_count, block_rows, feature_count)

    def column_sums(running, query_tile_rows):
        exponentials = exponent(query_tile_rows, columns)
        return (running + jnp.sum(exponentials, axis=0), jnp.sum(exponentials, axis=1))

    column_part, row_parts = lax.scan(
        column_sums, jnp.zeros((column_count,), jnp.float32), query_blocks
    )
    row_total = taken_together(row_parts.reshape(team_rows), INNER)
    column_total = lax.psum(column_part, "team")
    query_tile_rows = team_queries
    loss_weight = weights(query_tile_rows, columns, target_column, row_total, column_total)
    query_grad = summed_rows(
        logit_scale_factor * jnp.dot(loss_weight, columns, preferred_element_type=jnp.float32),
        INNER,
    )
    loss_weight = weights(team_queries, columns, target_column, row_total, column_total)
    passage_grad = summed_on_arrival(
        (
            logit_scale_factor
            * lax.dot_general(
                loss_weight,
                team_queries,
                (((0,), (0,)), ((), ())),
                preferred_element_type=jnp.float32,
            )
        ).astype(jnp.bfloat16),
        "team",
        0,
    )
    grad_queries = finish(query_unit, query_length, query_grad)
    grad_passages = finish(passage_unit, passage_length, passage_grad)
    return (grad_queries, grad_passages)


def solution(mesh):
    finer = Mesh(mesh.devices.reshape(mesh.shape["team"], 4, 4), ("team", "inner_0", "inner_1"))
    in_specs = (P(TEAM_INNER, None), P(TEAM_INNER, None), P(TEAM_INNER))
    out_specs = (P(TEAM_INNER, None), P(TEAM_INNER, None))
    return jax.shard_map(
        per_device, mesh=finer, in_specs=in_specs, out_specs=out_specs, check_vma=False
    )
```

profile of v0, /device:TPU:0, one launch (start us, length us, event | category | flops | bytes accessed | tf_op | source)
XLA Modules:
  0.0 193.5 jit_solution(252195710733847977)
XLA Ops:
  7.2 1.2 multiply_reduce_fusion.2
  8.4 1.9 fusion.18
  10.3 1.2 multiply_reduce_fusion.1
  11.4 1.1 fusion.17
  12.6 1.6 broadcast_in_dim.16
  14.2 4.4 %all-to-all-start = ((bf16[8,128,1024]{2,1,0:T(8,128)(2,1)}), bf16[8,128,1024]{2,1,0:T(8,128)(2,1)S(1)}, u32[]{:S(2)}, u32[]{:S(2)}) async-start(bf16[8,128,1024]{2,1,0:T(8,128)(2,1)} %broadcast_in_dim.16), calls=%async_computation | async-start | bytes 4194304 | tf_op jit(solution)/shard_map/all_to_all | solution.py:21
  18.6 22.2 %all-gather = s32[16,1,128]{2,1,0:T(1,128)S(1)} all-gather(s32[1,1,128]{2,1,0:T(1,128)S(1)} %bitcast.32), channel_id=1, replica_groups=mesh['team'=8,'inner_0'=4,'inner_1'=4] {'inner_0','inner_1'}, dimensions={0}, use_global_device_ids=true | all-gather | bytes 8704 | tf_op jit(solution)/shard_map/all_gather | solution.py:91
  40.8 5.0 %all-to-all-done = bf16[8,128,1024]{2,1,0:T(8,128)(2,1)S(1)} async-done(((bf16[8,128,1024]{2,1,0:T(8,128)(2,1)}), bf16[8,128,1024]{2,1,0:T(8,128)(2,1)S(1)}, u32[]{:S(2)}, u32[]{:S(2)}) %all-to-all-start) | async-done | bytes 2097184 | tf_op jit(solution)/shard_map/all_to_all | solution.py:21
  45.8 19.0 %all-gather.3.cloned.1.call-done = bf16[2048,1024]{1,0:T(8,128)(2,1)} async-done(((bf16[128,1024]{1,0:T(8,128)(2,1)}), bf16[2048,1024]{1,0:T(8,128)(2,1)}) %all-gather.3.cloned.1.call-update) | async-done | bytes 4194320 | tf_op jit(solution)/shard_map/all_gather | solution.py:90
  64.7 11.1 %while.13 = (s32[]{:T(128)}, f32[1024]{0:T(1024)S(1)}, f32[4,512]{1,0:T(4,128)S(1)}, bf16[4,512,1024]{2,1,0:T(8,128)(2,1)}, bf16[1024,1024]{1,0:T(8,128)(2,1)S(1)}, /*index=5*/s32[]{:T(128)}, s32[]{:T(128)}) while((s32[]{:T(128)}, f32[1024]{0:T(1024)S(1)}, f32[4,512]{1,0:T(4,128)S(1)}, bf16[4,512,1024]{2,1,0:T(8,128)(2,1)}, ...), condition=%wide.region_5.6_spmd.clone, body=%wide.region_2.5_spmd.clone.sunk | while | flops 1075315200 | bytes 3168359 | solution.py:106
  64.7 2.7 %fusion.29 = (f32[512]{0:T(512)S(1)}, f32[1024]{0:T(1024)S(1)}) fusion(bf16[1024,1024]{1,0:T(8,128)(2,1)S(1)} %get-tuple-element.115, bf16[4,512,1024]{2,1,0:T(8,128)(2,1)} %get-tuple-element.114, s32[]{:T(128)S(6)} %copy.12), kind=kOutput, calls=%fused_computation.1.clone.1 | convolution fusion | flops 1075313152 | bytes 3151876 | tf_op jit(solution)/shard_map/while/body/eval_jaxpr/dot_general | solution.py:63
  67.5 2.7 %fusion.29 = (f32[512]{0:T(512)S(1)}, f32[1024]{0:T(1024)S(1)}) fusion(bf16[1024,1024]{1,0:T(8,128)(2,1)S(1)} %get-tuple-element.115, bf16[4,512,1024]{2,1,0:T(8,128)(2,1)} %get-tuple-element.114, s32[]{:T(128)S(6)} %copy.12), kind=kOutput, calls=%fused_computation.1.clone.1 | convolution fusion | flops 1075313152 | bytes 3151876 | tf_op jit(solution)/shard_map/while/body/eval_jaxpr/dot_general | solution.py:63
  70.2 0.1 dynamic_update_slice.6
  70.3 2.7 %fusion.29 = (f32[512]{0:T(512)S(1)}, f32[1024]{0:T(1024)S(1)}) fusion(bf16[1024,1024]{1,0:T(8,128)(2,1)S(1)} %get-tuple-element.115, bf16[4,512,1024]{2,1,0:T(8,128)(2,1)} %get-tuple-element.114, s32[]{:T(128)S(6)} %copy.12), kind=kOutput, calls=%fused_computation.1.clone.1 | convolution fusion | flops 1075313152 | bytes 3151876 | tf_op jit(solution)/shard_map/while/body/eval_jaxpr/dot_general | solution.py:63
  73.1 2.7 %fusion.29 = (f32[512]{0:T(512)S(1)}, f32[1024]{0:T(1024)S(1)}) fusion(bf16[1024,1024]{1,0:T(8,128)(2,1)S(1)} %get-tuple-element.115, bf16[4,512,1024]{2,1,0:T(8,128)(2,1)} %get-tuple-element.114, s32[]{:T(128)S(6)} %copy.12), kind=kOutput, calls=%fused_computation.1.clone.1 | convolution fusion | flops 1075313152 | bytes 3151876 | tf_op jit(solution)/shard_map/while/body/eval_jaxpr/dot_general | solution.py:63
  75.8 0.1 dynamic_update_slice.6
  75.9 0.7 broadcast_in_dim.36
  76.6 5.3 %all-to-all-start.1 = ((f32[16,1,2048]{2,1,0:T(1,128)}), f32[16,1,2048]{2,1,0:T(1,128)S(1)}, u32[]{:S(2)}, u32[]{:S(2)}) async-start(f32[16,1,2048]{2,1,0:T(1,128)} %broadcast_in_dim.36), calls=%async_computation.1 | async-start | bytes 262144 | tf_op jit(solution)/shard_map/all_to_all | solution.py:21
  82.0 14.4 %psum.7 = f32[1024]{0:T(1024)S(1)} all-reduce(f32[1024]{0:T(1024)S(1)} %get-tuple-element.31), channel_id=1, replica_groups=mesh['team'=8,'inner_0'=4,'inner_1'=4] {'team'}, use_global_device_ids=true, to_apply=%region_7.8 | all-reduce | flops 1024 | bytes 8192 | tf_op jit(solution)/shard_map/psum | solution.py:110
  96.4 0.1 reduce_sum.74
  96.5 7.9 %subtract_convert_fusion = bf16[2048,1024]{1,0:T(8,128)(2,1)S(1)} fusion(bf16[2048,1024]{1,0:T(8,128)(2,1)} %bitcast.34, bf16[1024,1024]{1,0:T(8,128)(2,1)S(1)} %get-tuple-element.125, s32[2048]{0:T(1024)S(1)} %fusion.12, f32[1024]{0:T(1024)S(1)} %psum.7, f32[2048]{0:T(1024)S(1)} %reduce_sum.74), kind=kOutput, calls=%fused_computation.9 | convolution fusion | flops 4311744512 | bytes 10506240 | tf_op jit(solution)/shard_map/dot_general | solution.py:63
  104.4 2.0 %copy-done.3 = bf16[2048,1024]{1,0:T(8,128)(2,1)} copy-done((bf16[2048,1024]{1,0:T(8,128)(2,1)}, bf16[2048,1024]{1,0:T(8,128)(2,1)S(1)}, u32[]{:S(2)}) %copy-start.3) | copy-done | bytes 4194328
  106.4 6.1 %multiply_convert_fusion = bf16[2048,1024]{1,0:T(8,128)(2,1)} fusion(bf16[2048,1024]{1,0:T(8,128)(2,1)S(1)} %subtract_convert_fusion, bf16[1024,1024]{1,0:T(8,128)(2,1)S(1)} %get-tuple-element.125), kind=kOutput, calls=%fused_computation.8 | convolution fusion | flops 4299161600 | bytes 10485760 | tf_op jit(solution)/shard_map/dot_general | solution.py:114
  112.5 9.4 %multiply_convert_fusion.1 = bf16[1024,1024]{1,0:T(8,128)(2,1)} fusion(bf16[2048,1024]{1,0:T(8,128)(2,1)} %copy-done.3, bf16[2048,1024]{1,0:T(8,128)(2,1)} %bitcast.35), kind=kOutput, calls=%fused_computation.12 | convolution fusion | flops 4297064448 | bytes 10485760 | tf_op jit(solution)/shard_map/dot_general | solution.py:121
  121.9 3.7 %all-to-all-start.2 = ((bf16[8,128,1024]{2,1,0:T(8,128)(2,1)}), bf16[8,128,1024]{2,1,0:T(8,128)(2,1)S(1)}, u32[]{:S(2)}, u32[]{:S(2)}) async-start(bf16[8,128,1024]{2,1,0:T(8,128)(2,1)} %bitcast.27), calls=%async_computation.4 | async-start | bytes 4194304 | tf_op jit(solution)/shard_map/all_to_all | solution.py:48
  125.7 32.5 %reduce-scatter.3.cloned.1.call-done = bf16[512,1024]{1,0:T(8,128)(2,1)} async-done(((bf16[2048,1024]{1,0:T(8,128)(2,1)}), bf16[512,1024]{1,0:T(8,128)(2,1)}) %reduce-scatter.3.cloned.1.call-update) | async-done | bytes 1048592 | tf_op jit(solution)/shard_map/reduce_scatter | solution.py:36
  158.2 0.4 convert_reduce_fusion
  158.6 0.2 multiply_reduce_fusion
  158.8 1.0 subtract_divide_fusion
  159.8 24.1 %reduce-scatter.5.cloned.1.call-done = bf16[128,1024]{1,0:T(8,128)(2,1)} async-done(((bf16[512,1024]{1,0:T(8,128)(2,1)}), bf16[128,1024]{1,0:T(8,128)(2,1)}) %reduce-scatter.5.cloned.1.call-update) | async-done | bytes 262160 | tf_op jit(solution)/shard_map/reduce_scatter | solution.py:36
  183.9 1.2 fusion.6
  185.1 1.9 fusion.7
  (27 shorter events, 0.4 us)
Async XLA Ops:
  7.2 57.6 %all-gather.3.cloned.1.call-start = ((), (), s32[]{:S(2)}) async-start(), calls=%async_computation.5 | async-start | bytes 4456448 | tf_op jit(solution)/shard_map/all_gather | solution.py:90
  10.2 8.4 %copy-start.2 = (s32[128]{0:T(128)S(1)}, s32[128]{0:T(128)}, u32[]{:S(2)}) copy-start(s32[128]{0:T(128)} %param.7) | copy-start | bytes 1540
  14.2 31.6 %all-to-all-start = ((bf16[8,128,1024]{2,1,0:T(8,128)(2,1)}), bf16[8,128,1024]{2,1,0:T(8,128)(2,1)S(1)}, u32[]{:S(2)}, u32[]{:S(2)}) async-start(bf16[8,128,1024]{2,1,0:T(8,128)(2,1)} %broadcast_in_dim.16), calls=%async_computation | async-start | bytes 4194304 | tf_op jit(solution)/shard_map/all_to_all | solution.py:21
  76.6 19.8 %all-to-all-start.1 = ((f32[16,1,2048]{2,1,0:T(1,128)}), f32[16,1,2048]{2,1,0:T(1,128)S(1)}, u32[]{:S(2)}, u32[]{:S(2)}) async-start(f32[16,1,2048]{2,1,0:T(1,128)} %broadcast_in_dim.36), calls=%async_computation.1 | async-start | bytes 262144 | tf_op jit(solution)/shard_map/all_to_all | solution.py:21
  81.9 76.3 %reduce-scatter.3.cloned.1.call-start = ((), (), s32[]{:S(2)}) async-start(), calls=%async_computation.6 | async-start | bytes 5242880 | tf_op jit(solution)/shard_map/reduce_scatter | solution.py:36
  104.4 2.0 %copy-start.3 = (bf16[2048,1024]{1,0:T(8,128)(2,1)}, bf16[2048,1024]{1,0:T(8,128)(2,1)S(1)}, u32[]{:S(2)}) copy-start(bf16[2048,1024]{1,0:T(8,128)(2,1)S(1)} %subtract_convert_fusion) | copy-start | bytes 12582916
  121.9 36.7 %copy-start = (f32[128,1024]{1,0:T(8,128)S(1)}, f32[128,1024]{1,0:T(8,128)}, u32[]{:S(2)}) copy-start(f32[128,1024]{1,0:T(8,128)} %param.6) | copy-start | bytes 1572868
  121.9 36.3 %all-to-all-start.2 = ((bf16[8,128,1024]{2,1,0:T(8,128)(2,1)}), bf16[8,128,1024]{2,1,0:T(8,128)(2,1)S(1)}, u32[]{:S(2)}, u32[]{:S(2)}) async-start(bf16[8,128,1024]{2,1,0:T(8,128)(2,1)} %bitcast.27), calls=%async_computation.4 | async-start | bytes 4194304 | tf_op jit(solution)/shard_map/all_to_all | solution.py:48
  125.6 58.3 %copy-start.1 = (f32[128,1024]{1,0:T(8,128)S(1)}, f32[128,1024]{1,0:T(8,128)}, u32[]{:S(2)}) copy-start(f32[128,1024]{1,0:T(8,128)} %param.5) | copy-start | bytes 1572868
  125.6 58.3 %reduce-scatter.5.cloned.1.call-start = ((), (), s32[]{:S(2)}) async-start(), calls=%async_computation.7 | async-start | bytes 1310720 | tf_op jit(solution)/shard_map/reduce_scatter | solution.py:36
Sparse Core Ops, SparseCore 0:
  10.7 54.0 all-gather.2
  112.6 45.5 reduce-scatter.2
  160.6 23.2 reduce-scatter.4
where the time goes:
time: 194 us
  waiting for transfers between devices  80.6 us (42%)
  blocking collectives  36.5 us (19%)
  matrix products  34.2 us (18%)
  between operations  13.9 us (7%)
  starting transfers between devices  13.6 us (7%)
  other arithmetic  10.1 us (5%)
  local copies, waits for them, and re-layouts  4.51 us (2%)
    reduce_scatter x2, waiting for transfers between devices, summed_rows(): so_far = lax.psum_scatter(so_far, axis, scatter_dimension=0, tiled=True)  56.6 us
    all_gather x1, blocking collectives, per_device(): team_targets = lax.all_gather(positive, INNER, axis=0, tiled=True)  22.2 us
    all_gather x1, waiting for transfers between devices, per_device(): team_queries = lax.all_gather(query_round, INNER, axis=0, tiled=True)  19 us
    dot_general x5, matrix products, exponent(): lax.dot_general(query_tile_rows, column_block, (((1,), (1,)), ((), ())),...  18.8 us
    psum x1, blocking collectives, per_device(): column_total = lax.psum(column_part, 'team')  14.4 us
    all_to_all x2, starting transfers between devices, sent_to_all(): return lax.all_to_all(copies, axis, split_axis=0, concat_axis=0, tiled=True)  9.7 us
    dot_general x1, matrix products, per_device(): lax.dot_general(loss_weight, team_queries, (((0,), (0,)), ((), ())), pref...  9.41 us
    dot_general x1, matrix products, per_device(): jnp.dot(loss_weight, columns, preferred_element_type=jnp.float32)  6.06 us
  transfers between devices with their start and end apart: 6, of which 4 were waited for; matrix products, arithmetic and copies ran while one was open for 8% of the time, Pallas kernels for 0%

commit v1 on v0

--- a/solution.py
+++ b/solution.py
@@ -87,7 +87,10 @@
     passage_unit, passage_length = unit_rows(passages)
     query_round = query_unit.astype(jnp.bfloat16)
     passage_round = passage_unit.astype(jnp.bfloat16)
-    team_queries = lax.all_gather(query_round, INNER, axis=0, tiled=True)
+    n_dev = lax.axis_size(INNER)
+    pieces = jnp.stack([query_round for _ in range(n_dev)])
+    pieces = lax.all_to_all(pieces, INNER, split_axis=0, concat_axis=0)
+    team_queries = jnp.concatenate(pieces, axis=0)
     team_targets = lax.all_gather(positive, INNER, axis=0, tiled=True)
     columns = gathered_copies(passage_round, "team", 0)
     team_rows = shard_rows * inner_count

time: 194 us -> 257 us (1.32)
  blocking collectives: 36.5 us -> 86.7 us
  starting transfers between devices: 13.6 us -> 20.9 us
  matrix products: 34.2 us -> 37.6 us
  waiting for transfers between devices: 80.6 us -> 83.9 us
  other arithmetic: 10.1 us -> 7.36 us
    all_gather x1, blocking collectives: 22.2 us -> 73.8 us  [per_device(): team_targets = lax.all_gather(positive, INNER, axis=0, tiled=True)]
    all_to_all x2, waiting for transfers between devices: 5 us -> 26.9 us  [sent_to_all(): return lax.all_to_all(copies, axis, split_axis=0, concat_axis=0, tiled=True)]
    all_gather x1 -> x0, waiting for transfers between devices: 19 us -> none  [per_device(): team_queries = lax.all_gather(query_round, INNER, axis=0, tiled=True)]
    all_to_all x0 -> x1, starting transfers between devices: none -> 8.23 us  [per_device(): pieces = lax.all_to_all(pieces, INNER, split_axis=0, concat_axis=0)]
  transfers between devices with their start and end apart: 6 -> 6, of which waited for: 4 -> 3; matrix products, arithmetic and copies ran while one was open for 8% -> 4% of each run, Pallas kernels for 0% -> 0%
where the time goes in v1:
time: 257 us; the launch traced here: 256 us
  blocking collectives  86.7 us (34%)
  waiting for transfers between devices  83.9 us (33%)
  matrix products  37.6 us (15%)
  starting transfers between devices  20.9 us (8%)
  between operations  14.2 us (6%)
  other arithmetic  7.36 us (3%)
  local copies, waits for them, and re-layouts  5.06 us (2%)
    all_gather x1, blocking collectives, per_device(): team_targets = lax.all_gather(positive, INNER, axis=0, tiled=True)  73.8 us
    reduce_scatter x2, waiting for transfers between devices, summed_rows(): so_far = lax.psum_scatter(so_far, axis, scatter_dimension=0, tiled=True)  56.9 us
    all_to_all x2, waiting for transfers between devices, sent_to_all(): return lax.all_to_all(copies, axis, split_axis=0, concat_axis=0, tiled=True)  26.9 us
    dot_general x5, matrix products, exponent(): lax.dot_general(query_tile_rows, column_block, (((1,), (1,)), ((), ())),...  19.9 us
    psum x1, blocking collectives, per_device(): column_total = lax.psum(column_part, 'team')  12.9 us
    dot_general x1, matrix products, per_device(): lax.dot_general(loss_weight, team_queries, (((0,), (0,)), ((), ())), pref...  9.41 us
    all_to_all x2, starting transfers between devices, sent_to_all(): return lax.all_to_all(copies, axis, split_axis=0, concat_axis=0, tiled=True)  8.89 us
    dot_general x1, matrix products, per_device(): jnp.dot(loss_weight, columns, preferred_element_type=jnp.float32)  8.29 us
  transfers between devices with their start and end apart: 6, of which 3 were waited for; matrix products, arithmetic and copies ran while one was open for 4% of the time, Pallas kernels for 0%

profile of v1, /device:TPU:0, one launch (start us, length us, event | category | flops | bytes accessed | tf_op | source)
XLA Modules:
  0.0 255.8 jit_solution(5467014862202731772)
XLA Ops:
  7.2 1.2 multiply_reduce_fusion.1
  8.4 1.1 fusion.17
  9.6 1.6 broadcast_in_dim.16
  11.2 4.4 %all-to-all-start.1 = ((bf16[8,128,1024]{2,1,0:T(8,128)(2,1)}), bf16[8,128,1024]{2,1,0:T(8,128)(2,1)S(1)}, u32[]{:S(2)}, u32[]{:S(2)}) async-start(bf16[8,128,1024]{2,1,0:T(8,128)(2,1)} %broadcast_in_dim.16), calls=%async_computation.1 | async-start | bytes 4194304 | tf_op jit(solution)/shard_map/all_to_all | solution.py:21
  15.6 0.1 multiply_reduce_fusion.2
  15.7 0.1 fusion.18
  15.8 26.9 %all-to-all-done.1 = bf16[8,128,1024]{2,1,0:T(8,128)(2,1)S(1)} async-done(((bf16[8,128,1024]{2,1,0:T(8,128)(2,1)}), bf16[8,128,1024]{2,1,0:T(8,128)(2,1)S(1)}, u32[]{:S(2)}, u32[]{:S(2)}) %all-to-all-start.1) | async-done | bytes 2097184 | tf_op jit(solution)/shard_map/all_to_all | solution.py:21
  42.8 2.5 stack.2
  45.3 8.2 %all-to-all-start = ((bf16[16,128,1024]{2,1,0:T(8,128)(2,1)}), bf16[16,128,1024]{2,1,0:T(8,128)(2,1)}, u32[]{:S(2)}, u32[]{:S(2)}) async-start(bf16[16,128,1024]{2,1,0:T(8,128)(2,1)} %stack.2), calls=%async_computation | async-start | bytes 8388608 | tf_op jit(solution)/shard_map/all_to_all | solution.py:92
  53.5 73.8 %all-gather = s32[16,1,128]{2,1,0:T(1,128)S(1)} all-gather(s32[1,1,128]{2,1,0:T(1,128)S(1)} %bitcast.33), channel_id=1, replica_groups=mesh['team'=8,'inner_0'=4,'inner_1'=4] {'inner_0','inner_1'}, dimensions={0}, use_global_device_ids=true | all-gather | bytes 8704 | tf_op jit(solution)/shard_map/all_gather | solution.py:94
  127.4 10.9 %while.13 = (s32[]{:T(128)}, f32[1024]{0:T(1024)S(1)}, f32[4,512]{1,0:T(4,128)S(1)}, bf16[4,512,1024]{2,1,0:T(8,128)(2,1)}, bf16[1024,1024]{1,0:T(8,128)(2,1)S(1)}, /*index=5*/s32[]{:T(128)}, s32[]{:T(128)}) while((s32[]{:T(128)}, f32[1024]{0:T(1024)S(1)}, f32[4,512]{1,0:T(4,128)S(1)}, bf16[4,512,1024]{2,1,0:T(8,128)(2,1)}, ...), condition=%wide.region_5.6_spmd.clone, body=%wide.region_2.5_spmd.clone.sunk | while | flops 1075315200 | bytes 3168359 | solution.py:109
  127.4 2.7 %fusion.29 = (f32[512]{0:T(512)S(1)}, f32[1024]{0:T(1024)S(1)}) fusion(bf16[1024,1024]{1,0:T(8,128)(2,1)S(1)} %get-tuple-element.115, bf16[4,512,1024]{2,1,0:T(8,128)(2,1)} %get-tuple-element.114, s32[]{:T(128)S(6)} %copy.12), kind=kOutput, calls=%fused_computation.1.clone.1 | convolution fusion | flops 1075313152 | bytes 3151876 | tf_op jit(solution)/shard_map/while/body/eval_jaxpr/dot_general | solution.py:63
  130.0 0.1 dynamic_update_slice.6
  130.1 2.7 %fusion.29 = (f32[512]{0:T(512)S(1)}, f32[1024]{0:T(1024)S(1)}) fusion(bf16[1024,1024]{1,0:T(8,128)(2,1)S(1)} %get-tuple-element.115, bf16[4,512,1024]{2,1,0:T(8,128)(2,1)} %get-tuple-element.114, s32[]{:T(128)S(6)} %copy.12), kind=kOutput, calls=%fused_computation.1.clone.1 | convolution fusion | flops 1075313152 | bytes 3151876 | tf_op jit(solution)/shard_map/while/body/eval_jaxpr/dot_general | solution.py:63
  132.8 0.1 dynamic_update_slice.6
  132.8 2.7 %fusion.29 = (f32[512]{0:T(512)S(1)}, f32[1024]{0:T(1024)S(1)}) fusion(bf16[1024,1024]{1,0:T(8,128)(2,1)S(1)} %get-tuple-element.115, bf16[4,512,1024]{2,1,0:T(8,128)(2,1)} %get-tuple-element.114, s32[]{:T(128)S(6)} %copy.12), kind=kOutput, calls=%fused_computation.1.clone.1 | convolution fusion | flops 1075313152 | bytes 3151876 | tf_op jit(solution)/shard_map/while/body/eval_jaxpr/dot_general | solution.py:63
  135.6 2.7 %fusion.29 = (f32[512]{0:T(512)S(1)}, f32[1024]{0:T(1024)S(1)}) fusion(bf16[1024,1024]{1,0:T(8,128)(2,1)S(1)} %get-tuple-element.115, bf16[4,512,1024]{2,1,0:T(8,128)(2,1)} %get-tuple-element.114, s32[]{:T(128)S(6)} %copy.12), kind=kOutput, calls=%fused_computation.1.clone.1 | convolution fusion | flops 1075313152 | bytes 3151876 | tf_op jit(solution)/shard_map/while/body/eval_jaxpr/dot_general | solution.py:63
  138.3 0.7 broadcast_in_dim.36
  139.0 4.5 %all-to-all-start.2 = ((f32[16,1,2048]{2,1,0:T(1,128)}), f32[16,1,2048]{2,1,0:T(1,128)S(1)}, u32[]{:S(2)}, u32[]{:S(2)}) async-start(f32[16,1,2048]{2,1,0:T(1,128)} %broadcast_in_dim.36), calls=%async_computation.2 | async-start | bytes 262144 | tf_op jit(solution)/shard_map/all_to_all | solution.py:21
  143.6 12.9 %psum.7 = f32[1024]{0:T(1024)S(1)} all-reduce(f32[1024]{0:T(1024)S(1)} %get-tuple-element.31), channel_id=1, replica_groups=mesh['team'=8,'inner_0'=4,'inner_1'=4] {'team'}, use_global_device_ids=true, to_apply=%region_7.8 | all-reduce | flops 1024 | bytes 8192 | tf_op jit(solution)/shard_map/psum | solution.py:113
  156.5 0.1 reduce_sum.74
  156.6 9.3 %subtract_convert_fusion = bf16[2048,1024]{1,0:T(8,128)(2,1)} fusion(bf16[2048,1024]{1,0:T(8,128)(2,1)} %bitcast, bf16[1024,1024]{1,0:T(8,128)(2,1)S(1)} %get-tuple-element.126, s32[2048]{0:T(1024)S(1)} %fusion.12, f32[1024]{0:T(1024)S(1)} %psum.7, f32[2048]{0:T(1024)S(1)} %reduce_sum.74), kind=kOutput, calls=%fused_computation.9 | convolution fusion | flops 4311744512 | bytes 10506240 | tf_op jit(solution)/shard_map/dot_general | solution.py:63
  165.9 8.3 %multiply_convert_fusion = bf16[2048,1024]{1,0:T(8,128)(2,1)} fusion(bf16[2048,1024]{1,0:T(8,128)(2,1)} %subtract_convert_fusion, bf16[1024,1024]{1,0:T(8,128)(2,1)S(1)} %get-tuple-element.126), kind=kOutput, calls=%fused_computation.8 | convolution fusion | flops 4299161600 | bytes 10485760 | tf_op jit(solution)/shard_map/dot_general | solution.py:117
  174.2 9.4 %multiply_convert_fusion.1 = bf16[1024,1024]{1,0:T(8,128)(2,1)} fusion(bf16[2048,1024]{1,0:T(8,128)(2,1)} %subtract_convert_fusion, bf16[2048,1024]{1,0:T(8,128)(2,1)} %bitcast), kind=kOutput, calls=%fused_computation.12 | convolution fusion | flops 4297064448 | bytes 10485760 | tf_op jit(solution)/shard_map/dot_general | solution.py:124
  183.6 3.7 %all-to-all-start.3 = ((bf16[8,128,1024]{2,1,0:T(8,128)(2,1)}), bf16[8,128,1024]{2,1,0:T(8,128)(2,1)S(1)}, u32[]{:S(2)}, u32[]{:S(2)}) async-start(bf16[8,128,1024]{2,1,0:T(8,128)(2,1)} %bitcast.28), calls=%async_computation.5 | async-start | bytes 4194304 | tf_op jit(solution)/shard_map/all_to_all | solution.py:48
  187.4 32.8 %reduce-scatter.3.cloned.1.call-done = bf16[512,1024]{1,0:T(8,128)(2,1)} async-done(((bf16[2048,1024]{1,0:T(8,128)(2,1)}), bf16[512,1024]{1,0:T(8,128)(2,1)}) %reduce-scatter.3.cloned.1.call-update) | async-done | bytes 1048592 | tf_op jit(solution)/shard_map/reduce_scatter | solution.py:36
  220.2 0.3 convert_reduce_fusion
  220.6 0.2 multiply_reduce_fusion
  220.8 1.0 subtract_divide_fusion
  221.8 24.1 %reduce-scatter.5.cloned.1.call-done = bf16[128,1024]{1,0:T(8,128)(2,1)} async-done(((bf16[512,1024]{1,0:T(8,128)(2,1)}), bf16[128,1024]{1,0:T(8,128)(2,1)}) %reduce-scatter.5.cloned.1.call-update) | async-done | bytes 262160 | tf_op jit(solution)/shard_map/reduce_scatter | solution.py:36
  245.9 1.2 fusion.6
  247.1 1.9 fusion.7
  (25 shorter events, 0.3 us)
Async XLA Ops:
  7.2 8.4 %copy-start.1 = (f32[128,1024]{1,0:T(8,128)S(1)}, f32[128,1024]{1,0:T(8,128)}, u32[]{:S(2)}) copy-start(f32[128,1024]{1,0:T(8,128)} %param.5) | copy-start | bytes 1572868
  11.2 31.6 %all-to-all-start.1 = ((bf16[8,128,1024]{2,1,0:T(8,128)(2,1)}), bf16[8,128,1024]{2,1,0:T(8,128)(2,1)S(1)}, u32[]{:S(2)}, u32[]{:S(2)}) async-start(bf16[8,128,1024]{2,1,0:T(8,128)(2,1)} %broadcast_in_dim.16), calls=%async_computation.1 | async-start | bytes 4194304 | tf_op jit(solution)/shard_map/all_to_all | solution.py:21
  45.3 8.3 %copy-start.2 = (s32[128]{0:T(128)S(1)}, s32[128]{0:T(128)}, u32[]{:S(2)}) copy-start(s32[128]{0:T(128)} %param.7) | copy-start | bytes 1540
  45.3 82.1 %all-to-all-start = ((bf16[16,128,1024]{2,1,0:T(8,128)(2,1)}), bf16[16,128,1024]{2,1,0:T(8,128)(2,1)}, u32[]{:S(2)}, u32[]{:S(2)}) async-start(bf16[16,128,1024]{2,1,0:T(8,128)(2,1)} %stack.2), calls=%async_computation | async-start | bytes 8388608 | tf_op jit(solution)/shard_map/all_to_all | solution.py:92
  139.0 17.5 %all-to-all-start.2 = ((f32[16,1,2048]{2,1,0:T(1,128)}), f32[16,1,2048]{2,1,0:T(1,128)S(1)}, u32[]{:S(2)}, u32[]{:S(2)}) async-start(f32[16,1,2048]{2,1,0:T(1,128)} %broadcast_in_dim.36), calls=%async_computation.2 | async-start | bytes 262144 | tf_op jit(solution)/shard_map/all_to_all | solution.py:21
  143.5 76.7 %reduce-scatter.3.cloned.1.call-start = ((), (), s32[]{:S(2)}) async-start(), calls=%async_computation.6 | async-start | bytes 5242880 | tf_op jit(solution)/shard_map/reduce_scatter | solution.py:36
  183.6 37.0 %copy-start = (f32[128,1024]{1,0:T(8,128)S(1)}, f32[128,1024]{1,0:T(8,128)}, u32[]{:S(2)}) copy-start(f32[128,1024]{1,0:T(8,128)} %param.6) | copy-start | bytes 1572868
  183.6 36.6 %all-to-all-start.3 = ((bf16[8,128,1024]{2,1,0:T(8,128)(2,1)}), bf16[8,128,1024]{2,1,0:T(8,128)(2,1)S(1)}, u32[]{:S(2)}, u32[]{:S(2)}) async-start(bf16[8,128,1024]{2,1,0:T(8,128)(2,1)} %bitcast.28), calls=%async_computation.5 | async-start | bytes 4194304 | tf_op jit(solution)/shard_map/all_to_all | solution.py:48
  187.3 58.6 %reduce-scatter.5.cloned.1.call-start = ((), (), s32[]{:S(2)}) async-start(), calls=%async_computation.7 | async-start | bytes 1310720 | tf_op jit(solution)/shard_map/reduce_scatter | solution.py:36
Sparse Core Ops, SparseCore 0:
  174.3 45.8 reduce-scatter.2
  222.6 23.2 reduce-scatter.4
